TPU v7x, 32 devices: a whole 2x2x4 slice. The times are simulated.
32 devices in a mesh: node: 16 (over z, y, x), hand: 2 (over core).
Axes of the slice: x: 2, y: 2, z: 4, core: 2. Of those that a mesh axis runs over, the one named last changes fastest.
Arguments:
- ranges: bfloat16 [512, 128, 1326], P('node', None, 'hand'), may hold values from 0.00019931793 to 0.0039978027
- strengths: int32 [512, 1326], P('node'), may hold values from 0 to 399
- live_hands: int32 [512, 1326], P('node'), may hold values 0 or 1
- pot_sizes: float32 [512, 128], P('node'), may hold values from 1 to 16
- action_counts: int32 [512], P('node'), may hold values from 1 to 8
- parents: int32 [512], P('node'), may hold values from 0 to 63
- turn_counts: int32 [16], replicated, may hold values from 1 to 4
- root_reach: float32 [16, 2, 1326], P(None, None, 'hand'), may hold values from 0.01 to 1
Outputs:
- turn_values: float32 [16, 2, 1326], P('node', None, 'hand')
- exploitability: float32 [], replicated
All inputs are finite; a program needn't handle non-finite values. No bound on the sum of `live_hands` on one device may be relied on, other than what follows from the above.
Results may differ from a plain program's by a relative error of at most 0.0003.
Values may be sent and summed in bfloat16 or wider, within the bound.
A program may use at most 128 MiB of HBM per device.

v0:
```python
import jax
import jax.numpy as jnp
import numpy as np
from jax import lax
from jax.sharding import PartitionSpec as P

ACT = 8
GROUPS = 8
TACT = 4


def card_pairs(wanted):
    first_list = []
    second_list = []
    for lower_card in range(52):
        for upper_card in range(lower_card + 1, 52):
            first_list.append(lower_card)
            second_list.append(upper_card)
    return (
        jnp.asarray(np.array(first_list[:wanted], dtype=np.int32)),
        jnp.asarray(np.array(second_list[:wanted], dtype=np.int32)),
    )


def pair_compat(row_first, row_second, col_first, col_second):
    shared = (row_first[:, None] == col_first[None, :]) | (
        row_first[:, None] == col_second[None, :]
    )
    shared = (
        shared
        | (row_second[:, None] == col_first[None, :])
        | (row_second[:, None] == col_second[None, :])
    )
    return jnp.where(shared, 0.0, 1.0).astype(jnp.float32)


def showdown_block(compat, packed):
    left_strength, left_live, right_strength, right_live, reach_block = packed
    signs = jnp.sign((left_strength[:, :, None] - right_strength[:, None, :]).astype(jnp.float32))
    matrix = (signs * compat[None] * left_live[:, :, None] * right_live[:, None, :]).astype(
        jnp.bfloat16
    )
    return jnp.einsum("nij,nlj->nli", matrix, reach_block, preferred_element_type=jnp.float32)


def river_from(raw_values, pots, legal):
    count = raw_values.shape[0]
    width = raw_values.shape[2]
    values = (raw_values * pots[:, :, None]).reshape(count, 2, GROUPS, ACT, width)
    usable = jnp.arange(ACT)[None, :] < legal[:, None]
    return jnp.where(usable[:, None, None, :, None], values, -1e30).max(axis=3).sum(axis=2)


def turn_best(sums, legal):
    hand_half = sums.shape[1] // 2
    shaped = sums.reshape(-1, TACT, 2, hand_half)
    usable = jnp.arange(TACT)[None, :] < legal[:, None]
    return jnp.where(usable[:, :, None, None], shaped, -1e30).max(axis=1)


def local(
    ranges, strengths, live_hands, pot_sizes, action_counts, parents, turn_counts, root_reach
):
    node_count, line_cols, hand_half = ranges.shape
    hands_all = strengths.shape[1]
    hand_start = lax.axis_index("hand") * hand_half
    first_card, second_card = card_pairs(hands_all)
    live_all = live_hands.astype(jnp.float32)
    blocks = node_count // 4

    def grouped(array):
        return array.reshape((blocks, 4) + array.shape[1:])

    row_first = lax.dynamic_slice_in_dim(first_card, hand_start, hand_half, 0)
    row_second = lax.dynamic_slice_in_dim(second_card, hand_start, hand_half, 0)
    row_strength = lax.dynamic_slice_in_dim(strengths, hand_start, hand_half, 1)
    row_live = lax.dynamic_slice_in_dim(live_all, hand_start, hand_half, 1)
    compat = pair_compat(row_first, row_second, first_card, second_card)

    def one_block(packed):
        return showdown_block(compat, packed)

    added = lax.map(
        one_block,
        (
            grouped(row_strength),
            grouped(row_live),
            grouped(strengths),
            grouped(live_all),
            grouped(lax.all_gather(ranges, "hand", axis=2, tiled=True)),
        ),
    )
    raw_values = added.reshape(jnp.zeros((node_count, line_cols, hand_half), jnp.float32).shape)
    river_best = river_from(raw_values, pot_sizes, action_counts)
    flat_best = river_best.reshape(node_count, 2 * hand_half)
    turns_all = turn_counts.shape[0]
    turns_mine = turns_all // lax.axis_size("node")
    turn_start = lax.axis_index("node") * turns_mine
    parents_all = turns_all * TACT
    onehot = (parents[None, :] == jnp.arange(parents_all, dtype=jnp.int32)[:, None]).astype(
        jnp.float32
    )
    local_sums = jnp.dot(onehot, flat_best, precision=lax.Precision.HIGHEST)
    totals = lax.psum(local_sums, "node")
    values_all = turn_best(totals, turn_counts)
    exploitability = lax.psum(jnp.sum(root_reach * values_all), "hand")
    turn_values = lax.dynamic_slice_in_dim(values_all, turn_start, turns_mine, 0)
    return (turn_values, exploitability)


def solution(mesh):
    in_specs = (
        P("node", None, "hand"),
        P("node", None),
        P("node", None),
        P("node", None),
        P("node"),
        P("node"),
        P(),
        P(None, None, "hand"),
    )
    out_specs = (P("node", None, "hand"), P())
    return jax.shard_map(local, mesh=mesh, in_specs=in_specs, out_specs=out_specs, check_vma=False)
```

profile of v0, /device:TPU:0, one launch (start us, length us, event | category | flops | bytes accessed | tf_op | source)
XLA Modules:
  0.0 278.7 jit_solution(3800787151186367840)
XLA Ops:
  14.4 20.9 %all-gather.2.cloned.1.call-done = bf16[32,128,1326]{1,0,2:T(8,128)(2,1)} async-done(((bf16[32,128,663]{1,0,2:T(8,128)(2,1)}), bf16[32,128,1326]{1,0,2:T(8,128)(2,1)}) %all-gather.2.cloned.1.call-update) | async-done | bytes 10862608 | tf_op jit(solution)/shard_map/all_gather | solution.py:90
  35.3 89.9 %while.11 = (s32[]{:T(128)}, f32[8,4,128,663]{2,3,1,0:T(8,128)}, bf16[8,4,128,1326]{2,1,0,3:T(4,128)(2,1)}, s32[8,4,663]{2,1,0:T(4,128)S(1)}, s32[8,4,1326]{2,1,...) while((s32[]{:T(128)}, f32[8,4,128,663]{2,3,1,0:T(8,128)}, ...), condition=%wide.region_1.2_spmd.clone, body=%wide.region_0.1_spmd.clone.sunk | while | flops 931886272 | bytes 12673953 | solution.py:83
  35.3 1.6 constant_dynamic-slice_fusion.5
  37.0 2.2 or_select_fusion.2
  39.2 7.4 %fusion.9 = f32[8,4,128,663]{2,3,1,0:T(8,128)} fusion(f32[8,4,128,663]{2,3,1,0:T(8,128)} %get-tuple-element.197, s32[]{:T(128)} %get-tuple-element.196, f32[4,1326]{1,0:T(4,128)S(1)} %dynamic-slice_bitcast_fusion.8, f32[4,663]{1,0:T(4,128)S(1)} %dynamic-slice_bitcast_fusion.9, f32[663,1326]{1,0:T(8,128)S(1)} %or_select_fusion.2, ...), kind=kOutput, calls=%fused_computation.5.clone.1 | convolution fusion | flops 924853184 | bytes 6298408 | tf_op jit(solution)/shard_map/while/body/eval_jaxpr/nij,nlj->nli/dot_general | solution.py:43
  46.6 1.6 constant_dynamic-slice_fusion.5
  48.3 2.2 or_select_fusion.2
  50.5 7.3 %fusion.9 = f32[8,4,128,663]{2,3,1,0:T(8,128)} fusion(f32[8,4,128,663]{2,3,1,0:T(8,128)} %get-tuple-element.197, s32[]{:T(128)} %get-tuple-element.196, f32[4,1326]{1,0:T(4,128)S(1)} %dynamic-slice_bitcast_fusion.8, f32[4,663]{1,0:T(4,128)S(1)} %dynamic-slice_bitcast_fusion.9, f32[663,1326]{1,0:T(8,128)S(1)} %or_select_fusion.2, ...), kind=kOutput, calls=%fused_computation.5.clone.1 | convolution fusion | flops 924853184 | bytes 6298408 | tf_op jit(solution)/shard_map/while/body/eval_jaxpr/nij,nlj->nli/dot_general | solution.py:43
  57.8 1.6 constant_dynamic-slice_fusion.5
  59.5 2.2 or_select_fusion.2
  61.7 7.3 %fusion.9 = f32[8,4,128,663]{2,3,1,0:T(8,128)} fusion(f32[8,4,128,663]{2,3,1,0:T(8,128)} %get-tuple-element.197, s32[]{:T(128)} %get-tuple-element.196, f32[4,1326]{1,0:T(4,128)S(1)} %dynamic-slice_bitcast_fusion.8, f32[4,663]{1,0:T(4,128)S(1)} %dynamic-slice_bitcast_fusion.9, f32[663,1326]{1,0:T(8,128)S(1)} %or_select_fusion.2, ...), kind=kOutput, calls=%fused_computation.5.clone.1 | convolution fusion | flops 924853184 | bytes 6298408 | tf_op jit(solution)/shard_map/while/body/eval_jaxpr/nij,nlj->nli/dot_general | solution.py:43
  69.0 1.6 constant_dynamic-slice_fusion.5
  70.7 2.2 or_select_fusion.2
  73.0 7.3 %fusion.9 = f32[8,4,128,663]{2,3,1,0:T(8,128)} fusion(f32[8,4,128,663]{2,3,1,0:T(8,128)} %get-tuple-element.197, s32[]{:T(128)} %get-tuple-element.196, f32[4,1326]{1,0:T(4,128)S(1)} %dynamic-slice_bitcast_fusion.8, f32[4,663]{1,0:T(4,128)S(1)} %dynamic-slice_bitcast_fusion.9, f32[663,1326]{1,0:T(8,128)S(1)} %or_select_fusion.2, ...), kind=kOutput, calls=%fused_computation.5.clone.1 | convolution fusion | flops 924853184 | bytes 6298408 | tf_op jit(solution)/shard_map/while/body/eval_jaxpr/nij,nlj->nli/dot_general | solution.py:43
  80.2 1.6 constant_dynamic-slice_fusion.5
  81.9 2.2 or_select_fusion.2
  84.2 7.3 %fusion.9 = f32[8,4,128,663]{2,3,1,0:T(8,128)} fusion(f32[8,4,128,663]{2,3,1,0:T(8,128)} %get-tuple-element.197, s32[]{:T(128)} %get-tuple-element.196, f32[4,1326]{1,0:T(4,128)S(1)} %dynamic-slice_bitcast_fusion.8, f32[4,663]{1,0:T(4,128)S(1)} %dynamic-slice_bitcast_fusion.9, f32[663,1326]{1,0:T(8,128)S(1)} %or_select_fusion.2, ...), kind=kOutput, calls=%fused_computation.5.clone.1 | convolution fusion | flops 924853184 | bytes 6298408 | tf_op jit(solution)/shard_map/while/body/eval_jaxpr/nij,nlj->nli/dot_general | solution.py:43
  91.5 1.6 constant_dynamic-slice_fusion.5
  93.2 2.2 or_select_fusion.2
  95.4 7.3 %fusion.9 = f32[8,4,128,663]{2,3,1,0:T(8,128)} fusion(f32[8,4,128,663]{2,3,1,0:T(8,128)} %get-tuple-element.197, s32[]{:T(128)} %get-tuple-element.196, f32[4,1326]{1,0:T(4,128)S(1)} %dynamic-slice_bitcast_fusion.8, f32[4,663]{1,0:T(4,128)S(1)} %dynamic-slice_bitcast_fusion.9, f32[663,1326]{1,0:T(8,128)S(1)} %or_select_fusion.2, ...), kind=kOutput, calls=%fused_computation.5.clone.1 | convolution fusion | flops 924853184 | bytes 6298408 | tf_op jit(solution)/shard_map/while/body/eval_jaxpr/nij,nlj->nli/dot_general | solution.py:43
  102.7 1.6 constant_dynamic-slice_fusion.5
  104.4 2.2 or_select_fusion.2
  106.7 7.3 %fusion.9 = f32[8,4,128,663]{2,3,1,0:T(8,128)} fusion(f32[8,4,128,663]{2,3,1,0:T(8,128)} %get-tuple-element.197, s32[]{:T(128)} %get-tuple-element.196, f32[4,1326]{1,0:T(4,128)S(1)} %dynamic-slice_bitcast_fusion.8, f32[4,663]{1,0:T(4,128)S(1)} %dynamic-slice_bitcast_fusion.9, f32[663,1326]{1,0:T(8,128)S(1)} %or_select_fusion.2, ...), kind=kOutput, calls=%fused_computation.5.clone.1 | convolution fusion | flops 924853184 | bytes 6298408 | tf_op jit(solution)/shard_map/while/body/eval_jaxpr/nij,nlj->nli/dot_general | solution.py:43
  113.9 1.6 constant_dynamic-slice_fusion.5
  115.6 2.2 or_select_fusion.2
  117.9 7.3 %fusion.9 = f32[8,4,128,663]{2,3,1,0:T(8,128)} fusion(f32[8,4,128,663]{2,3,1,0:T(8,128)} %get-tuple-element.197, s32[]{:T(128)} %get-tuple-element.196, f32[4,1326]{1,0:T(4,128)S(1)} %dynamic-slice_bitcast_fusion.8, f32[4,663]{1,0:T(4,128)S(1)} %dynamic-slice_bitcast_fusion.9, f32[663,1326]{1,0:T(8,128)S(1)} %or_select_fusion.2, ...), kind=kOutput, calls=%fused_computation.5.clone.1 | convolution fusion | flops 924853184 | bytes 6298408 | tf_op jit(solution)/shard_map/while/body/eval_jaxpr/nij,nlj->nli/dot_general | solution.py:43
  125.2 12.0 %copy.22 = f32[8,4,128,663]{3,2,1,0:T(8,128)} copy(f32[8,4,128,663]{2,3,1,0:T(8,128)} %get-tuple-element.44) | data formatting | bytes 21725184 | tf_op jit(solution)/shard_map/while | solution.py:83
  137.1 16.8 %select_reduce_fusion = f32[32,2,8,663]{3,2,1,0:T(8,128)S(1)} fusion(f32[32,2,8,8,663]{4,3,2,1,0:T(8,128)} %bitcast.31, f32[32,2,8,8]{3,2,1,0:T(8,128)S(1)} %copy.24, pred[32,8]{1,0:T(8,128)(4,1)S(1)} %iota_compare_fusion.2), kind=kLoop, calls=%fused_computation.12 | loop fusion | flops 7807488 | bytes 12237056 | tf_op jit(solution)/shard_map/reduce_max | solution.py:51
  154.9 1.1 reshape.95
  156.2 109.9 %all-reduce.2.cloned.1.call-done = f32[16,4,2,663]{3,2,1,0:T(2,128)} async-done(((f32[16,4,2,663]{3,2,1,0:T(2,128)}), f32[16,4,2,663]{3,2,1,0:T(2,128)}) %all-reduce.2.cloned.1.call-update) | async-done | bytes 339472 | tf_op jit(solution)/shard_map/psum | solution.py:104
  266.1 1.4 select_reduce_fusion.1
  268.8 3.1 %psum.15 = f32[]{:T(128)} all-reduce(f32[]{:T(128)} %multiply_reduce_fusion), channel_id=1, replica_groups=mesh['node'=16,'hand'=2] {'hand'}, use_global_device_ids=true, to_apply=%region_7.8 | all-reduce | flops 1 | bytes 8 | tf_op jit(solution)/shard_map/psum | solution.py:106
  (61 shorter events, 9.8 us)
Async XLA Ops:
  7.2 28.1 %all-gather.2.cloned.1.call-start = ((), (), s32[]{:S(2)}) async-start(), calls=%async_computation | async-start | bytes 16293888 | tf_op jit(solution)/shard_map/all_gather | solution.py:90
  7.9 258.2 %all-reduce.2.cloned.1.call-start = ((), (), s32[]{:S(2)}) async-start(), calls=%async_computation.1 | async-start | bytes 786432 | tf_op jit(solution)/shard_map/psum | solution.py:104
  137.1 17.5 %copy-start.1 = (s32[32]{0:T(128)S(1)}, s32[32]{0:T(128)}, u32[]{:S(2)}) copy-start(s32[32]{0:T(128)} %param.17) | copy-start | bytes 388
  137.1 18.9 %copy-start.2 = (s32[16]{0:T(128)S(1)}, s32[16]{0:T(128)}, u32[]{:S(2)}) copy-start(s32[16]{0:T(128)} %param.18) | copy-start | bytes 196
  137.1 130.4 %copy-start = (f32[16,2,663]{2,1,0:T(2,128)S(1)}, f32[16,2,663]{2,1,0:T(2,128)}, u32[]{:S(2)}) copy-start(f32[16,2,663]{2,1,0:T(2,128)} %param.19) | copy-start | bytes 254596
Sparse Core Ops, SparseCore 0:
  9.5 25.7 all-gather.1
  156.2 109.8 all-reduce.1
where the time goes:
time: 280 us; the launch traced here: 279 us
  waiting for transfers between devices  132 us (47%)
  matrix products  58.7 us (21%)
  other arithmetic  39.1 us (14%)
  local copies, waits for them, and re-layouts  31.7 us (11%)
  between operations  14.2 us (5%)
  blocking collectives  3.08 us (1%)
    psum x1, waiting for transfers between devices, local(): totals = lax.psum(local_sums, 'node')  110 us
    dot_general x8, matrix products, showdown_block(): jnp.einsum('nij,nlj->nli', matrix, reach_block, preferred_element_type=jn...  58.4 us
    all_gather x1, waiting for transfers between devices, local(): lax.all_gather(ranges, 'hand', axis=2, tiled=True)  20.9 us
    select_n x8, other arithmetic, pair_compat(): return jnp.where(shared, 0.0, 1.0).astype(jnp.float32)  17.9 us
    reduce_max x1, other arithmetic, river_from(): jnp.where(usable[:, None, None, :, None], values, -1e+30).max(axis=3)  16.8 us
    dynamic_slice x8, local copies, waits for them, and re-layouts, local(): lax.map(one_block, (grouped(row_strength), grouped(row_live), grouped(str...  12.8 us
    while x1, local copies, waits for them, and re-layouts, local(): lax.map(one_block, (grouped(row_strength), grouped(row_live), grouped(str...  12 us
  transfers between devices with their start and end apart: 2, of which 2 were waited for; matrix products, arithmetic and copies ran while one was open for 2% of the time, Pallas kernels for 0%

commit v1 on v0

--- a/solution.py
+++ b/solution.py
@@ -3,10 +3,12 @@
 import numpy as np
 from jax import lax
 from jax.sharding import PartitionSpec as P
+from jax.lax import all_gather
 
 ACT = 8
 GROUPS = 8
 TACT = 4
+fix_target = lambda t0: all_gather(t0, axis_name="node").sum(axis=0)
 
 
 def card_pairs(wanted):
@@ -101,7 +103,7 @@
         jnp.float32
     )
     local_sums = jnp.dot(onehot, flat_best, precision=lax.Precision.HIGHEST)
-    totals = lax.psum(local_sums, "node")
+    totals = fix_target(local_sums)
     values_all = turn_best(totals, turn_counts)
     exploitability = lax.psum(jnp.sum(root_reach * values_all), "hand")
     turn_values = lax.dynamic_slice_in_dim(values_all, turn_start, turns_mine, 0)

time: 280 us -> 262 us (0.936)
  waiting for transfers between devices: 132 us -> 112 us
    psum x1 -> x0, waiting for transfers between devices: 110 us -> none  [local(): totals = lax.psum(local_sums, 'node')]
    all_gather x0 -> x1, waiting for transfers between devices: none -> 90 us  [fix_target = lambda t0: all_gather(t0, axis_name='node').sum(axis=0)]
    reduce_sum x0 -> x1, other arithmetic: none -> 2.95 us  [fix_target = lambda t0: all_gather(t0, axis_name='node').sum(axis=0)]
where the time goes in v1:
time: 262 us; the launch traced here: 261 us
  waiting for transfers between devices  112 us (43%)
  matrix products  59.4 us (23%)
  other arithmetic  40.9 us (16%)
  local copies, waits for them, and re-layouts  31 us (12%)
  between operations  14.2 us (5%)
  blocking collectives  3.08 us (1%)
    all_gather x1, waiting for transfers between devices, fix_target = lambda t0: all_gather(t0, axis_name='node').sum(axis=0)  90 us
    dot_general x8, matrix products, showdown_block(): jnp.einsum('nij,nlj->nli', matrix, reach_block, preferred_element_type=jn...  58.4 us
    all_gather x1, waiting for transfers between devices, local(): lax.all_gather(ranges, 'hand', axis=2, tiled=True)  20.9 us
    select_n x8, other arithmetic, pair_compat(): return jnp.where(shared, 0.0, 1.0).astype(jnp.float32)  17.9 us
    reduce_max x1, other arithmetic, river_from(): jnp.where(usable[:, None, None, :, None], values, -1e+30).max(axis=3)  16.8 us
    dynamic_slice x8, local copies, waits for them, and re-layouts, local(): lax.map(one_block, (grouped(row_strength), grouped(row_live), grouped(str...  12.8 us
    while x1, local copies, waits for them, and re-layouts, local(): lax.map(one_block, (grouped(row_strength), grouped(row_live), grouped(str...  12 us
  transfers between devices with their start and end apart: 2, of which 2 were waited for; matrix products, arithmetic and copies ran while one was open for 2% of the time, Pallas kernels for 0%

profile of v1, /device:TPU:0, one launch (start us, length us, event | category | flops | bytes accessed | tf_op | source)
XLA Modules:
  0.0 260.6 jit_solution(15740748312715223570)
XLA Ops:
  14.4 20.9 %all-gather.4.cloned.1.call-done = bf16[32,128,1326]{1,0,2:T(8,128)(2,1)} async-done(((bf16[32,128,663]{1,0,2:T(8,128)(2,1)}), bf16[32,128,1326]{1,0,2:T(8,128)(2,1)}) %all-gather.4.cloned.1.call-update) | async-done | bytes 10862608 | tf_op jit(solution)/shard_map/all_gather | solution.py:92
  35.3 89.9 %while.11 = (s32[]{:T(128)}, f32[8,4,128,663]{2,3,1,0:T(8,128)}, bf16[8,4,128,1326]{2,1,0,3:T(4,128)(2,1)}, s32[8,4,663]{2,1,0:T(4,128)S(1)}, s32[8,4,1326]{2,1,...) while((s32[]{:T(128)}, f32[8,4,128,663]{2,3,1,0:T(8,128)}, ...), condition=%wide.region_1.2_spmd.clone, body=%wide.region_0.1_spmd.clone.sunk | while | flops 931886272 | bytes 12673953 | solution.py:85
  35.3 1.6 constant_dynamic-slice_fusion.5
  37.0 2.2 or_select_fusion.2
  39.2 7.3 %fusion.10 = f32[8,4,128,663]{2,3,1,0:T(8,128)} fusion(f32[8,4,128,663]{2,3,1,0:T(8,128)} %get-tuple-element.214, s32[]{:T(128)} %get-tuple-element.213, f32[4,1326]{1,0:T(4,128)S(1)} %dynamic-slice_bitcast_fusion.8, f32[4,663]{1,0:T(4,128)S(1)} %dynamic-slice_bitcast_fusion.9, f32[663,1326]{1,0:T(8,128)S(1)} %or_select_fusion.2, ...), kind=kOutput, calls=%fused_computation.5.clone.1 | convolution fusion | flops 924853184 | bytes 6298408 | tf_op jit(solution)/shard_map/while/body/eval_jaxpr/nij,nlj->nli/dot_general | solution.py:45
  46.6 1.6 constant_dynamic-slice_fusion.5
  48.3 2.2 or_select_fusion.2
  50.5 7.3 %fusion.10 = f32[8,4,128,663]{2,3,1,0:T(8,128)} fusion(f32[8,4,128,663]{2,3,1,0:T(8,128)} %get-tuple-element.214, s32[]{:T(128)} %get-tuple-element.213, f32[4,1326]{1,0:T(4,128)S(1)} %dynamic-slice_bitcast_fusion.8, f32[4,663]{1,0:T(4,128)S(1)} %dynamic-slice_bitcast_fusion.9, f32[663,1326]{1,0:T(8,128)S(1)} %or_select_fusion.2, ...), kind=kOutput, calls=%fused_computation.5.clone.1 | convolution fusion | flops 924853184 | bytes 6298408 | tf_op jit(solution)/shard_map/while/body/eval_jaxpr/nij,nlj->nli/dot_general | solution.py:45
  57.8 1.6 constant_dynamic-slice_fusion.5
  59.5 2.2 or_select_fusion.2
  61.7 7.3 %fusion.10 = f32[8,4,128,663]{2,3,1,0:T(8,128)} fusion(f32[8,4,128,663]{2,3,1,0:T(8,128)} %get-tuple-element.214, s32[]{:T(128)} %get-tuple-element.213, f32[4,1326]{1,0:T(4,128)S(1)} %dynamic-slice_bitcast_fusion.8, f32[4,663]{1,0:T(4,128)S(1)} %dynamic-slice_bitcast_fusion.9, f32[663,1326]{1,0:T(8,128)S(1)} %or_select_fusion.2, ...), kind=kOutput, calls=%fused_computation.5.clone.1 | convolution fusion | flops 924853184 | bytes 6298408 | tf_op jit(solution)/shard_map/while/body/eval_jaxpr/nij,nlj->nli/dot_general | solution.py:45
  69.0 1.6 constant_dynamic-slice_fusion.5
  70.7 2.2 or_select_fusion.2
  73.0 7.3 %fusion.10 = f32[8,4,128,663]{2,3,1,0:T(8,128)} fusion(f32[8,4,128,663]{2,3,1,0:T(8,128)} %get-tuple-element.214, s32[]{:T(128)} %get-tuple-element.213, f32[4,1326]{1,0:T(4,128)S(1)} %dynamic-slice_bitcast_fusion.8, f32[4,663]{1,0:T(4,128)S(1)} %dynamic-slice_bitcast_fusion.9, f32[663,1326]{1,0:T(8,128)S(1)} %or_select_fusion.2, ...), kind=kOutput, calls=%fused_computation.5.clone.1 | convolution fusion | flops 924853184 | bytes 6298408 | tf_op jit(solution)/shard_map/while/body/eval_jaxpr/nij,nlj->nli/dot_general | solution.py:45
  80.2 1.6 constant_dynamic-slice_fusion.5
  81.9 2.2 or_select_fusion.2
  84.2 7.3 %fusion.10 = f32[8,4,128,663]{2,3,1,0:T(8,128)} fusion(f32[8,4,128,663]{2,3,1,0:T(8,128)} %get-tuple-element.214, s32[]{:T(128)} %get-tuple-element.213, f32[4,1326]{1,0:T(4,128)S(1)} %dynamic-slice_bitcast_fusion.8, f32[4,663]{1,0:T(4,128)S(1)} %dynamic-slice_bitcast_fusion.9, f32[663,1326]{1,0:T(8,128)S(1)} %or_select_fusion.2, ...), kind=kOutput, calls=%fused_computation.5.clone.1 | convolution fusion | flops 924853184 | bytes 6298408 | tf_op jit(solution)/shard_map/while/body/eval_jaxpr/nij,nlj->nli/dot_general | solution.py:45
  91.5 1.6 constant_dynamic-slice_fusion.5
  93.2 2.2 or_select_fusion.2
  95.4 7.3 %fusion.10 = f32[8,4,128,663]{2,3,1,0:T(8,128)} fusion(f32[8,4,128,663]{2,3,1,0:T(8,128)} %get-tuple-element.214, s32[]{:T(128)} %get-tuple-element.213, f32[4,1326]{1,0:T(4,128)S(1)} %dynamic-slice_bitcast_fusion.8, f32[4,663]{1,0:T(4,128)S(1)} %dynamic-slice_bitcast_fusion.9, f32[663,1326]{1,0:T(8,128)S(1)} %or_select_fusion.2, ...), kind=kOutput, calls=%fused_computation.5.clone.1 | convolution fusion | flops 924853184 | bytes 6298408 | tf_op jit(solution)/shard_map/while/body/eval_jaxpr/nij,nlj->nli/dot_general | solution.py:45
  102.7 1.6 constant_dynamic-slice_fusion.5
  104.4 2.2 or_select_fusion.2
  106.6 7.3 %fusion.10 = f32[8,4,128,663]{2,3,1,0:T(8,128)} fusion(f32[8,4,128,663]{2,3,1,0:T(8,128)} %get-tuple-element.214, s32[]{:T(128)} %get-tuple-element.213, f32[4,1326]{1,0:T(4,128)S(1)} %dynamic-slice_bitcast_fusion.8, f32[4,663]{1,0:T(4,128)S(1)} %dynamic-slice_bitcast_fusion.9, f32[663,1326]{1,0:T(8,128)S(1)} %or_select_fusion.2, ...), kind=kOutput, calls=%fused_computation.5.clone.1 | convolution fusion | flops 924853184 | bytes 6298408 | tf_op jit(solution)/shard_map/while/body/eval_jaxpr/nij,nlj->nli/dot_general | solution.py:45
  113.9 1.6 constant_dynamic-slice_fusion.5
  115.6 2.2 or_select_fusion.2
  117.8 7.3 %fusion.10 = f32[8,4,128,663]{2,3,1,0:T(8,128)} fusion(f32[8,4,128,663]{2,3,1,0:T(8,128)} %get-tuple-element.214, s32[]{:T(128)} %get-tuple-element.213, f32[4,1326]{1,0:T(4,128)S(1)} %dynamic-slice_bitcast_fusion.8, f32[4,663]{1,0:T(4,128)S(1)} %dynamic-slice_bitcast_fusion.9, f32[663,1326]{1,0:T(8,128)S(1)} %or_select_fusion.2, ...), kind=kOutput, calls=%fused_computation.5.clone.1 | convolution fusion | flops 924853184 | bytes 6298408 | tf_op jit(solution)/shard_map/while/body/eval_jaxpr/nij,nlj->nli/dot_general | solution.py:45
  125.2 12.0 %copy.28 = f32[8,4,128,663]{3,2,1,0:T(8,128)} copy(f32[8,4,128,663]{2,3,1,0:T(8,128)} %get-tuple-element.44) | data formatting | bytes 21725184 | tf_op jit(solution)/shard_map/while | solution.py:85
  137.1 16.8 %select_reduce_fusion = f32[32,2,8,663]{3,2,1,0:T(8,128)S(1)} fusion(f32[32,2,8,8,663]{4,3,2,1,0:T(8,128)} %bitcast.32, f32[32,2,8,8]{3,2,1,0:T(8,128)S(1)} %copy.30, pred[32,8]{1,0:T(8,128)(4,1)S(1)} %iota_compare_fusion.2), kind=kLoop, calls=%fused_computation.12 | loop fusion | flops 7807488 | bytes 12237056 | tf_op jit(solution)/shard_map/reduce_max | solution.py:53
  154.6 1.0 fusion.6
  155.7 90.0 %all-gather.6.cloned.1.call-done = f32[1024,1326]{1,0:T(8,128)} async-done(((f32[64,1326]{1,0:T(8,128)}), f32[1024,1326]{1,0:T(8,128)}) %all-gather.6.cloned.1.call-update) | async-done | bytes 5431312 | tf_op jit(solution)/shard_map/all_gather | solution.py:11
  245.7 3.0 %reduce_sum.28 = f32[64,1326]{1,0:T(8,128)S(1)} reduce(f32[16,64,1326]{2,1,0:T(8,128)} %bitcast.33, f32[]{:T(128)} %constant.19.clone.1), dimensions={0}, to_apply=%region_4.5 | reduce | flops 1272960 | bytes 5770756 | tf_op jit(solution)/shard_map/reduce_sum | solution.py:11
  250.7 3.1 %psum.7 = f32[]{:T(128)} all-reduce(f32[]{:T(128)} %get-tuple-element.132), channel_id=1, replica_groups=mesh['node'=16,'hand'=2] {'hand'}, use_global_device_ids=true, to_apply=%region_7.8 | all-reduce | flops 1 | bytes 8 | tf_op jit(solution)/shard_map/psum | solution.py:108
  (63 shorter events, 10.3 us)
Async XLA Ops:
  7.2 28.1 %all-gather.4.cloned.1.call-start = ((), (), s32[]{:S(2)}) async-start(), calls=%async_computation | async-start | bytes 16293888 | tf_op jit(solution)/shard_map/all_gather | solution.py:92
  7.9 237.8 %all-gather.6.cloned.1.call-start = ((), (), s32[]{:S(2)}) async-start(), calls=%async_computation.1 | async-start | bytes 6127616 | tf_op jit(solution)/shard_map/all_gather | solution.py:11
  137.1 17.5 %copy-start.1 = (s32[32]{0:T(128)S(1)}, s32[32]{0:T(128)}, u32[]{:S(2)}) copy-start(s32[32]{0:T(128)} %param.17) | copy-start | bytes 388
  137.1 18.5 %copy-start.2 = (s32[16]{0:T(128)S(1)}, s32[16]{0:T(128)}, u32[]{:S(2)}) copy-start(s32[16]{0:T(128)} %param.18) | copy-start | bytes 196
  137.1 112.4 %copy-start = (f32[16,2,663]{2,1,0:T(2,128)S(1)}, f32[16,2,663]{2,1,0:T(2,128)}, u32[]{:S(2)}) copy-start(f32[16,2,663]{2,1,0:T(2,128)} %param.19) | copy-start | bytes 254596
Sparse Core Ops, SparseCore 0:
  9.5 25.7 all-gather.3
  155.8 89.9 all-gather.5
